TPU v7x, 512 devices: a whole 4x4x16 slice. The times are simulated.
512 devices in a mesh: grp: 16 (over z), dp: 32 (over x, y, core).
Axes of the slice: x: 4, y: 4, z: 16, core: 2. Of those that a mesh axis runs over, the one named last changes fastest.
Arguments:
- tokens: bfloat16 [65536, 3584], P(('grp', 'dp')), may hold values from -120 to 120, as said below
- lengths: int32 [512, 4], P(('grp', 'dp')), may hold values from 0 to 128, as said below
- dest: int32 [512, 4], P(('grp', 'dp')), may hold values from -1 to 15, as said below
- gain: float32 [3584], replicated, may hold values from 0.5 to 1.5
- weight: bfloat16 [3584, 10240], P('dp', 'grp'), may hold values from -0.09375 to 0.09375
Outputs:
- projected: bfloat16 [32768, 10240], P('dp', 'grp')
Inputs may be any that keep to these rules, and one draw needn't show every extreme that they name: The tokens of one row have a common scale, and so have those of one feature. A device's live rows are the sum of its lengths; rows after them are padding. Within the devices sharing a dp index, live rows fill ceil(live rows / 32) blocks on each device and 32 blocks in all. dest is -1 exactly for a device's blocks past its live rows and an owner along grp otherwise. Within the devices sharing a dp index, every owner receives exactly 2 blocks and no device sends more than 1 block to one owner.
All inputs are finite; a program needn't handle non-finite values.
Results may differ from a plain program's by a relative error of at most 0.0049.
Values may be sent and summed in bfloat16 or wider, within the bound.
No kernel may reach another device: no remote copies, remote signals or barrier semaphores. Data moves between devices by JAX's collectives and lax.ppermute only.
A program may use at most 64 MiB of HBM per device.

v0:
```python
import jax
import jax.numpy as jnp
from jax import lax
from jax.sharding import PartitionSpec as P

BLK = 32
OWN_BLK = 2
EPS = 1e-06


def in_one_piece(arrays, axis, dim, along):
    widths = [a.shape[along] for a in arrays]
    both = jnp.concatenate(arrays, axis=along)
    result = lax.all_gather(both, axis, axis=dim, tiled=True)
    return tuple(jnp.split(result, [sum(widths[:k]) for k in range(1, len(widths))], axis=along))


def group_layout(dest_all, own_blocks):
    groups, slots_in = dest_all.shape
    flat_dest = dest_all.reshape(-1)
    flat_index = jnp.arange(groups * slots_in, dtype=jnp.int32)
    earlier = flat_index[None, :] < flat_index[:, None]
    same_dest = flat_dest[:, None] == flat_dest[None, :]
    source = flat_index // slots_in
    owner_rank = jnp.sum((same_dest & earlier).astype(jnp.int32), axis=1)
    pair_rank = jnp.sum(
        (same_dest & earlier & (source[:, None] == source[None, :])).astype(jnp.int32), axis=1
    )
    matches = (flat_dest[:, None, None] == jnp.arange(groups, dtype=jnp.int32)[None, :, None]) & (
        owner_rank[:, None, None] == jnp.arange(own_blocks, dtype=jnp.int32)[None, None, :]
    )
    picked = jnp.sum(jnp.where(matches, flat_index[:, None, None], 0), axis=0)
    return (picked, pair_rank)


def local_onehot(lens_row, count):
    doc_ends = jnp.cumsum(lens_row)
    position = jnp.arange(count, dtype=jnp.int32)
    doc_index = jnp.sum((position[:, None] >= doc_ends[None, :]).astype(jnp.int32), axis=1)
    is_live = position < doc_ends[-1]
    return (
        doc_index[:, None] == jnp.arange(lens_row.shape[0], dtype=jnp.int32)[None, :]
    ) & is_live[:, None]


def doc_squares(rows, onehot):
    widened = rows.astype(jnp.float32)
    square = jnp.sum(widened * widened, axis=1)
    return jnp.sum(jnp.where(onehot, square[:, None], 0.0), axis=0)


def apply_scale(rows, onehot, totals, lens_flat, gain):
    features = rows.shape[1]
    mean_square = totals / (jnp.maximum(lens_flat, 1).astype(jnp.float32) * features)
    inverse = lax.rsqrt(mean_square + EPS)
    scale = jnp.sum(jnp.where(onehot, inverse[None, :], 0.0), axis=1)
    return (rows.astype(jnp.float32) * scale[:, None] * gain[None, :]).astype(jnp.bfloat16)


def fold_rows(rows_all, weight):
    return jnp.dot(
        rows_all,
        lax.all_gather(weight, "dp", axis=0, tiled=True),
        preferred_element_type=jnp.float32,
    ).astype(jnp.bfloat16)


def per_device(tokens, lengths, dest, gain, weight):
    groups = lax.axis_size("grp")
    slots_in = 2 * OWN_BLK
    features = tokens.shape[1]
    pair_most = max(1, (slots_in + groups - 1) // groups)
    lens_all, dest_all = in_one_piece((lengths, dest), "grp", 0, 1)
    picked, pair_rank = group_layout(dest_all, OWN_BLK)
    my_index = lax.axis_index("grp")
    my_blocks = lax.dynamic_index_in_dim(picked, my_index, 0, keepdims=False)
    source_onehot = local_onehot(lengths[0], tokens.shape[0])
    source_totals = doc_squares(tokens, source_onehot)
    outgoing = apply_scale(tokens, source_onehot, source_totals, lengths[0], gain)
    my_dest = dest[0]
    local_index = jnp.arange(slots_in, dtype=jnp.int32)
    my_pair = jnp.sum(
        (
            (my_dest[:, None] == my_dest[None, :]) & (local_index[None, :] < local_index[:, None])
        ).astype(jnp.int32),
        axis=1,
    )
    slot_ids = jnp.arange(groups * pair_most, dtype=jnp.int32)
    send_pick = (my_dest[None, :] == (slot_ids // pair_most)[:, None]) & (
        my_pair[None, :] == (slot_ids % pair_most)[:, None]
    )
    parcel = jnp.dot(
        send_pick.astype(jnp.bfloat16),
        outgoing.reshape(slots_in, BLK * features),
        preferred_element_type=jnp.float32,
    ).astype(jnp.bfloat16)
    arrived = lax.all_to_all(parcel, "grp", split_axis=0, concat_axis=0, tiled=True)
    take_slot = my_blocks // slots_in * pair_most + pair_rank[my_blocks]
    take_onehot = (take_slot[:, None] == slot_ids[None, :]).astype(jnp.bfloat16)
    owned_rows = jnp.dot(take_onehot, arrived, preferred_element_type=jnp.float32).astype(
        jnp.bfloat16
    )
    owned_rows = owned_rows.reshape(OWN_BLK * BLK, features)
    rows_all = lax.all_gather(owned_rows, "grp", axis=0, tiled=True)
    return fold_rows(rows_all, weight)


def solution(mesh):
    placed = (
        P(("grp", "dp"), None),
        P(("grp", "dp"), None),
        P(("grp", "dp"), None),
        P(),
        P("dp", "grp"),
    )
    return jax.shard_map(
        per_device, mesh=mesh, in_specs=placed, out_specs=P("dp", "grp"), check_vma=False
    )
```

profile of v0, /device:TPU:1, one launch (start us, length us, event | category | flops | bytes accessed | tf_op | source)
XLA Modules:
  0.0 362.2 jit_solution(12504840859904070301)
XLA Ops:
  6.5 0.8 reduce-window.4
  7.4 0.6 slice.4
  8.0 0.6 iota_compare_fusion.7
  8.7 1.4 fusion.3
  10.1 0.1 select_reduce_fusion.2
  10.3 0.7 rsqrt_bitcast_fusion
  11.0 1.5 fusion.5
  12.5 0.7 reshape.164
  13.2 0.2 convert_reduce_fusion.3
  13.4 2.9 fusion
  16.3 0.5 broadcast.230
  16.8 6.2 %reduce.3 = bf16[16,114688]{1,0:T(8,128)(2,1)} reduce(bf16[16,1,114688]{2,0,1:T(8,128)(2,1)} %fusion, bf16[]{:T(256)} %broadcast.230), dimensions={1}, to_apply=%copy.21.reduce_sub_computation | reduce | bytes 7340034 | tf_op jit(solution)/shard_map/all_to_all | solution.py:97
  23.0 5.9 %reshape.178 = bf16[16,2,57344]{2,1,0:T(2,128)(2,1)} reshape(bf16[16,114688]{1,0:T(8,128)(2,1)} %reduce.3) | data formatting | bytes 7340032
  28.9 15.9 %all-to-all-start = ((bf16[16,2,57344]{2,1,0:T(2,128)(2,1)}), bf16[16,2,57344]{2,1,0:T(2,128)(2,1)}, u32[]{:S(2)}, u32[]{:S(2)}) async-start(bf16[16,2,57344]{2,1,0:T(2,128)(2,1)} %reshape.178), calls=%async_computation | async-start | bytes 7340032 | tf_op jit(solution)/shard_map/all_to_all | solution.py:97
  44.9 0.7 all-gather.6.cloned.1.call-update
  45.7 176.0 %all-gather = s32[16,1,8]{2,1,0:T(1,128)S(1)} all-gather(s32[1,1,8]{2,1,0:T(1,128)S(1)} %add_bitcast_fusion), channel_id=1, replica_groups=mesh['grp'=16,'dp'=32] {'grp'}, dimensions={0}, use_global_device_ids=true | all-gather | bytes 544 | tf_op jit(solution)/shard_map/all_gather | solution.py:14
  222.0 0.2 convert_reduce_fusion.1
  222.3 0.2 dynamic-slice_reduce_fusion
  222.5 0.6 gather_fusion
  223.2 12.0 %reshape.179 = bf16[16,1,114688]{2,1,0:T(2,128)(2,1)} reshape(bf16[16,2,57344]{2,1,0:T(2,128)(2,1)} %all-to-all-done) | data formatting | bytes 7340032
  235.2 7.2 %convolution_convert_fusion.1 = bf16[2,114688]{1,0:T(2,128)(2,1)S(1)} fusion(bf16[16,1,114688]{2,1,0:T(2,128)(2,1)} %reshape.179, s32[2]{0:T(128)S(1)} %fusion.17), kind=kOutput, calls=%fused_computation.3 | convolution fusion | flops 7569440 | bytes 4128776 | tf_op jit(solution)/shard_map/dot_general | solution.py:100
  242.4 1.2 reshape.165
  243.7 101.4 %all-gather.4.cloned.1.call-done = bf16[1024,3584]{1,0:T(8,128)(2,1)} async-done(((bf16[64,3584]{1,0:T(8,128)(2,1)}), bf16[1024,3584]{1,0:T(8,128)(2,1)}) %all-gather.4.cloned.1.call-update) | async-done | bytes 7340048 | tf_op jit(solution)/shard_map/all_gather | solution.py:104
  345.1 10.3 %convolution_convert_fusion.2 = bf16[1024,640]{1,0:T(8,128)(2,1)} fusion(bf16[1024,3584]{1,0:T(8,128)(2,1)} %all-gather.4.cloned.1.call-done, bf16[3584,640]{1,0:T(8,128)(2,1)} %all-gather.6.cloned.1.call-done), kind=kOutput, calls=%fused_computation.11 | convolution fusion | flops 4698275840 | bytes 13238272 | tf_op jit(solution)/shard_map/dot_general | solution.py:61
  (24 shorter events, 0.8 us)
Async XLA Ops:
  6.5 6.6 %copy-start = (s32[1,4]{1,0:T(1,128)S(1)}, s32[1,4]{1,0:T(1,128)}, u32[]{:S(2)}) copy-start(s32[1,4]{1,0:T(1,128)} %param.7) | copy-start | bytes 52
  28.9 16.7 %copy-start.1 = (s32[1,4]{1,0:T(1,128)S(1)}, s32[1,4]{1,0:T(1,128)}, u32[]{:S(2)}) copy-start(s32[1,4]{1,0:T(1,128)} %param.6) | copy-start | bytes 52
  28.9 194.3 %all-to-all-start = ((bf16[16,2,57344]{2,1,0:T(2,128)(2,1)}), bf16[16,2,57344]{2,1,0:T(2,128)(2,1)}, u32[]{:S(2)}, u32[]{:S(2)}) async-start(bf16[16,2,57344]{2,1,0:T(2,128)(2,1)} %reshape.178), calls=%async_computation | async-start | bytes 7340032 | tf_op jit(solution)/shard_map/all_to_all | solution.py:97
  44.9 198.8 %all-gather.6.cloned.1.call-start = ((), (), s32[]{:S(2)}) async-start(), calls=%async_computation.2 | async-start | bytes 4730880 | tf_op jit(solution)/shard_map/all_gather | solution.py:63
  45.6 299.5 %all-gather.4.cloned.1.call-start = ((), (), s32[]{:S(2)}) async-start(), calls=%async_computation.1 | async-start | bytes 7798784 | tf_op jit(solution)/shard_map/all_gather | solution.py:104
Sparse Core Ops, SparseCore 0:
  48.9 63.6 all-gather.5
  243.7 101.3 all-gather.3
where the time goes:
time: 363 us; the launch traced here: 362 us
  blocking collectives  176 us (48%)
  waiting for transfers between devices  102 us (28%)
  local copies, waits for them, and re-layouts  22 us (6%)
  matrix products  20.3 us (6%)
  starting transfers between devices  16 us (4%)
  between operations  13.5 us (4%)
  other arithmetic  12.2 us (3%)
    all_gather x1, blocking collectives, in_one_piece(): result = lax.all_gather(both, axis, axis=dim, tiled=True)  176 us
    all_gather x1, waiting for transfers between devices, per_device(): rows_all = lax.all_gather(owned_rows, 'grp', axis=0, tiled=True)  101 us
    unnamed x6, local copies, waits for them, and re-layouts  18 us
    all_to_all x1, starting transfers between devices, per_device(): lax.all_to_all(parcel, 'grp', split_axis=0, concat_axis=0, tiled=True)  15.9 us
    dot_general x1, matrix products, fold_rows(): jnp.dot(rows_all, lax.all_gather(weight, 'dp', axis=0, tiled=True), prefe...  10.3 us
  transfers between devices with their start and end apart: 3, of which 1 were waited for; matrix products, arithmetic and copies ran while one was open for 6% of the time, Pallas kernels for 0%

commit v1 on v0

--- a/solution.py
+++ b/solution.py
@@ -6,6 +6,28 @@
 BLK = 32
 OWN_BLK = 2
 EPS = 1e-06
+
+
+def joined_along(pieces, dim):
+    lengths = list(pieces.shape[1:])
+    lengths[dim] *= pieces.shape[0]
+    return jnp.moveaxis(pieces, 0, dim).reshape(lengths)
+
+
+def ring_gather(array, axis, dim):
+    count = lax.axis_size(axis)
+    pairs = [(i, (i + 1) % count) for i in range(count)]
+    back = [(b, a) for a, b in pairs]
+    lower, upper = ([], [])
+    for step in range(count - 1):
+        if step % 2 == 0:
+            lower.append(lax.ppermute(lower[-1] if lower else array, axis, pairs))
+        else:
+            upper.append(lax.ppermute(upper[-1] if upper else array, axis, back))
+    blocks = jnp.stack([*lower[::-1], array, *upper])
+    shift = lax.axis_index(axis) - len(lower)
+    blocks = blocks[(jnp.arange(count) - shift) % count]
+    return joined_along(blocks, dim)
 
 
 def in_one_piece(arrays, axis, dim, along):
@@ -101,7 +123,7 @@
         jnp.bfloat16
     )
     owned_rows = owned_rows.reshape(OWN_BLK * BLK, features)
-    rows_all = lax.all_gather(owned_rows, "grp", axis=0, tiled=True)
+    rows_all = ring_gather(owned_rows, "grp", 0)
     return fold_rows(rows_all, weight)
 
 

time: 363 us -> 437 us (1.20)
  starting transfers between devices: 16 us -> 66.2 us
  local copies, waits for them, and re-layouts: 22 us -> 49.8 us
  waiting for transfers between devices: 102 us -> 95.5 us
    all_gather x1 -> x0, waiting for transfers between devices: 101 us -> none  [per_device(): rows_all = lax.all_gather(owned_rows, 'grp', axis=0, tiled=True)]
    ppermute x0 -> x15, waiting for transfers between devices: none -> 55.1 us  [the longest x8 53.3 us: ring_gather(): lower.append(lax.ppermute(lower[-1] if lower else array, axis, pairs))]
    ppermute x0 -> x15, starting transfers between devices: none -> 50.3 us  [the longest x7 34.6 us: ring_gather(): upper.append(lax.ppermute(upper[-1] if upper else array, axis, back))]
    all_gather x1, waiting for transfers between devices: 0.02 us -> 40.4 us  [fold_rows(): lax.all_gather(weight, 'dp', axis=0, tiled=True)]
    unnamed x6 -> x35, local copies, waits for them, and re-layouts: 18 us -> 38.2 us
    gather x0 -> x1, local copies, waits for them, and re-layouts: none -> 7.16 us  [ring_gather(): blocks = blocks[(jnp.arange(count) - shift) % count]]
  transfers between devices with their start and end apart: 3 -> 17, of which waited for: 1 -> 11; matrix products, arithmetic and copies ran while one was open for 6% -> 7% of each run, Pallas kernels for 0% -> 0%
where the time goes in v1:
time: 437 us; the launch traced here: 436 us
  blocking collectives  177 us (41%)
  waiting for transfers between devices  95.5 us (22%)
  starting transfers between devices  66.2 us (15%)
  local copies, waits for them, and re-layouts  49.8 us (11%)
  matrix products  21 us (5%)
  between operations  13.7 us (3%)
  other arithmetic  12.9 us (3%)
    all_gather x1, blocking collectives, in_one_piece(): result = lax.all_gather(both, axis, axis=dim, tiled=True)  177 us
    ppermute x8, waiting for transfers between devices, ring_gather(): lower.append(lax.ppermute(lower[-1] if lower else array, axis, pairs))  53.3 us
    all_gather x1, waiting for transfers between devices, fold_rows(): lax.all_gather(weight, 'dp', axis=0, tiled=True)  40.4 us
    unnamed x35, local copies, waits for them, and re-layouts  38.2 us
    ppermute x7, starting transfers between devices, ring_gather(): upper.append(lax.ppermute(upper[-1] if upper else array, axis, back))  34.6 us
    all_to_all x1, starting transfers between devices, per_device(): lax.all_to_all(parcel, 'grp', split_axis=0, concat_axis=0, tiled=True)  15.8 us
    ppermute x8, starting transfers between devices, ring_gather(): lower.append(lax.ppermute(lower[-1] if lower else array, axis, pairs))  15.7 us
    dot_general x1, matrix products, fold_rows(): jnp.dot(rows_all, lax.all_gather(weight, 'dp', axis=0, tiled=True), prefe...  10.3 us
  transfers between devices with their start and end apart: 17, of which 11 were waited for; matrix products, arithmetic and copies ran while one was open for 7% of the time, Pallas kernels for 0%

profile of v1, /device:TPU:1, one launch (start us, length us, event | category | flops | bytes accessed | tf_op | source)
XLA Modules:
  0.0 435.8 jit_solution(12506132122604426210)
XLA Ops:
  18.2 6.2 %reduce.3 = bf16[16,114688]{1,0:T(8,128)(2,1)} reduce(bf16[16,1,114688]{2,0,1:T(8,128)(2,1)} %fusion, bf16[]{:T(256)} %broadcast.298), dimensions={1}, to_apply=%copy.21.reduce_sub_computation | reduce | bytes 7340034 | tf_op jit(solution)/shard_map/all_to_all | solution.py:119
  24.4 6.0 %reshape.239 = bf16[16,2,57344]{2,1,0:T(2,128)(2,1)} reshape(bf16[16,114688]{1,0:T(8,128)(2,1)} %reduce.3) | data formatting | bytes 7340032
  30.4 15.8 %all-to-all-start = ((bf16[16,2,57344]{2,1,0:T(2,128)(2,1)}), bf16[16,2,57344]{2,1,0:T(2,128)(2,1)}, u32[]{:S(2)}, u32[]{:S(2)}) async-start(bf16[16,2,57344]{2,1,0:T(2,128)(2,1)} %reshape.239), calls=%async_computation | async-start | bytes 7340032 | tf_op jit(solution)/shard_map/all_to_all | solution.py:119
  46.3 176.7 %all-gather = s32[16,1,8]{2,1,0:T(1,128)S(1)} all-gather(s32[1,1,8]{2,1,0:T(1,128)S(1)} %add_bitcast_fusion), channel_id=1, replica_groups=mesh['grp'=16,'dp'=32] {'grp'}, dimensions={0}, use_global_device_ids=true | all-gather | bytes 544 | tf_op jit(solution)/shard_map/all_gather | solution.py:36
  224.5 12.0 %reshape.240 = bf16[16,1,114688]{2,1,0:T(2,128)(2,1)} reshape(bf16[16,2,57344]{2,1,0:T(2,128)(2,1)} %all-to-all-done) | data formatting | bytes 7340032
  236.6 7.2 %convolution_convert_fusion.1 = bf16[2,114688]{1,0:T(2,128)(2,1)S(1)} fusion(bf16[16,1,114688]{2,1,0:T(2,128)(2,1)} %reshape.240, s32[2]{0:T(128)S(1)} %fusion.19), kind=kOutput, calls=%fused_computation.4 | convolution fusion | flops 7569440 | bytes 4128776 | tf_op jit(solution)/shard_map/dot_general | solution.py:122
  246.5 8.1 %collective-permute-done = bf16[64,3584]{1,0:T(8,128)(2,1)S(1)} collective-permute-done((bf16[64,3584]{1,0:T(8,128)(2,1)S(1)}, bf16[64,3584]{1,0:T(8,128)(2,1)S(1)}, u32[]{:S(2)}, u32[]{:S(2)}) %collective-permute-start) | collective-permute-done | bytes 458784 | tf_op jit(solution)/shard_map/ppermute | solution.py:24
  256.5 4.6 %collective-permute-start.8 = (bf16[64,3584]{1,0:T(8,128)(2,1)S(1)}, bf16[64,3584]{1,0:T(8,128)(2,1)S(1)}, u32[]{:S(2)}, u32[]{:S(2)}) collective-permute-start(bf16[64,3584]{1,0:T(8,128)(2,1)S(1)} %reshape.217), channel_id=1, source_target_pairs={{32,0},{64,32},{96,64},{128,96},{160,128},{192,160},{224,192},{256... | collective-permute-start | bytes 1376264 | tf_op jit(solution)/shard_map/ppermute | solution.py:26
  261.1 6.0 %collective-permute-done.1 = bf16[64,3584]{1,0:T(8,128)(2,1)S(1)} collective-permute-done((bf16[64,3584]{1,0:T(8,128)(2,1)S(1)}, bf16[64,3584]{1,0:T(8,128)(2,1)S(1)}, u32[]{:S(2)}, u32[]{:S(2)}) %collective-permute-start.1) | collective-permute-done | bytes 458784 | tf_op jit(solution)/shard_map/ppermute | solution.py:24
  269.0 4.8 %collective-permute-start.9 = (bf16[64,3584]{1,0:T(8,128)(2,1)S(1)}, bf16[64,3584]{1,0:T(8,128)(2,1)S(1)}, u32[]{:S(2)}, u32[]{:S(2)}) collective-permute-start(bf16[64,3584]{1,0:T(8,128)(2,1)S(1)} %collective-permute-done.8), channel_id=1, source_target_pairs={{32,0},{64,32},{96,64},{128,96},{160,128},{192,160},{224,192},{256... | collective-permute-start | bytes 1376264 | tf_op jit(solution)/shard_map/ppermute | solution.py:26
  273.7 6.9 %collective-permute-done.2 = bf16[64,3584]{1,0:T(8,128)(2,1)S(1)} collective-permute-done((bf16[64,3584]{1,0:T(8,128)(2,1)S(1)}, bf16[64,3584]{1,0:T(8,128)(2,1)S(1)}, u32[]{:S(2)}, u32[]{:S(2)}) %collective-permute-start.2) | collective-permute-done | bytes 458784 | tf_op jit(solution)/shard_map/ppermute | solution.py:24
  282.6 4.8 %collective-permute-start.10 = (bf16[64,3584]{1,0:T(8,128)(2,1)S(1)}, bf16[64,3584]{1,0:T(8,128)(2,1)S(1)}, u32[]{:S(2)}, u32[]{:S(2)}) collective-permute-start(bf16[64,3584]{1,0:T(8,128)(2,1)S(1)} %collective-permute-done.9), channel_id=1, source_target_pairs={{32,0},{64,32},{96,64},{128,96},{160,128},{192,160},{224,192},{256... | collective-permute-start | bytes 1376264 | tf_op jit(solution)/shard_map/ppermute | solution.py:26
  287.4 8.0 %collective-permute-done.3 = bf16[64,3584]{1,0:T(8,128)(2,1)S(1)} collective-permute-done((bf16[64,3584]{1,0:T(8,128)(2,1)S(1)}, bf16[64,3584]{1,0:T(8,128)(2,1)S(1)}, u32[]{:S(2)}, u32[]{:S(2)}) %collective-permute-start.3) | collective-permute-done | bytes 458784 | tf_op jit(solution)/shard_map/ppermute | solution.py:24
  297.4 5.0 %collective-permute-start.11 = (bf16[64,3584]{1,0:T(8,128)(2,1)S(1)}, bf16[64,3584]{1,0:T(8,128)(2,1)S(1)}, u32[]{:S(2)}, u32[]{:S(2)}) collective-permute-start(bf16[64,3584]{1,0:T(8,128)(2,1)S(1)} %collective-permute-done.10), channel_id=1, source_target_pairs={{32,0},{64,32},{96,64},{128,96},{160,128},{192,160},{224,192},{256... | collective-permute-start | bytes 1376264 | tf_op jit(solution)/shard_map/ppermute | solution.py:26
  302.4 8.1 %collective-permute-done.4 = bf16[64,3584]{1,0:T(8,128)(2,1)S(1)} collective-permute-done((bf16[64,3584]{1,0:T(8,128)(2,1)S(1)}, bf16[64,3584]{1,0:T(8,128)(2,1)S(1)}, u32[]{:S(2)}, u32[]{:S(2)}) %collective-permute-start.4) | collective-permute-done | bytes 458784 | tf_op jit(solution)/shard_map/ppermute | solution.py:24
  313.2 4.8 %collective-permute-start.12 = (bf16[64,3584]{1,0:T(8,128)(2,1)S(1)}, bf16[64,3584]{1,0:T(8,128)(2,1)}, u32[]{:S(2)}, u32[]{:S(2)}) collective-permute-start(bf16[64,3584]{1,0:T(8,128)(2,1)S(1)} %collective-permute-done.11), channel_id=1, source_target_pairs={{32,0},{64,32},{96,64},{128,96},{160,128},{192,160},{224,192},{256... | collective-permute-start | bytes 1376264 | tf_op jit(solution)/shard_map/ppermute | solution.py:26
  318.1 6.6 %collective-permute-done.5 = bf16[64,3584]{1,0:T(8,128)(2,1)S(1)} collective-permute-done((bf16[64,3584]{1,0:T(8,128)(2,1)S(1)}, bf16[64,3584]{1,0:T(8,128)(2,1)S(1)}, u32[]{:S(2)}, u32[]{:S(2)}) %collective-permute-start.5) | collective-permute-done | bytes 458784 | tf_op jit(solution)/shard_map/ppermute | solution.py:24
  327.6 5.3 %collective-permute-start.13 = (bf16[64,3584]{1,0:T(8,128)(2,1)}, bf16[64,3584]{1,0:T(8,128)(2,1)}, u32[]{:S(2)}, u32[]{:S(2)}) collective-permute-start(bf16[64,3584]{1,0:T(8,128)(2,1)} %collective-permute-done.12), channel_id=1, source_target_pairs={{32,0},{64,32},{96,64},{128,96},{160,128},{192,160},{224,192},{256... | collective-permute-start | bytes 1376264 | tf_op jit(solution)/shard_map/ppermute | solution.py:26
  332.9 5.1 %collective-permute-done.6 = bf16[64,3584]{1,0:T(8,128)(2,1)} collective-permute-done((bf16[64,3584]{1,0:T(8,128)(2,1)S(1)}, bf16[64,3584]{1,0:T(8,128)(2,1)}, u32[]{:S(2)}, u32[]{:S(2)}) %collective-permute-start.6) | collective-permute-done | bytes 458784 | tf_op jit(solution)/shard_map/ppermute | solution.py:24
  341.3 5.3 %collective-permute-start.14 = (bf16[64,3584]{1,0:T(8,128)(2,1)}, bf16[64,3584]{1,0:T(8,128)(2,1)S(1)}, u32[]{:S(2)}, u32[]{:S(2)}) collective-permute-start(bf16[64,3584]{1,0:T(8,128)(2,1)} %collective-permute-done.13), channel_id=1, source_target_pairs={{32,0},{64,32},{96,64},{128,96},{160,128},{192,160},{224,192},{256... | collective-permute-start | bytes 1376264 | tf_op jit(solution)/shard_map/ppermute | solution.py:26
  346.6 4.5 %collective-permute-done.7 = bf16[64,3584]{1,0:T(8,128)(2,1)} collective-permute-done((bf16[64,3584]{1,0:T(8,128)(2,1)}, bf16[64,3584]{1,0:T(8,128)(2,1)}, u32[]{:S(2)}, u32[]{:S(2)}) %collective-permute-start.7) | collective-permute-done | bytes 458784 | tf_op jit(solution)/shard_map/ppermute | solution.py:24
  371.2 7.2 %gather_fusion.1 = bf16[16,64,3584]{2,1,0:T(8,128)(2,1)} fusion(bf16[16,64,3584]{2,1,0:T(8,128)(2,1)} %bitcast_dynamic-update-slice_fusion, s32[1024]{0:T(1024)S(1)} %pad_clamp_fusion), kind=kCustom, calls=%fused_computation.1 | custom fusion | bytes 14680128 | tf_op jit(solution)/shard_map/gather | solution.py:29
  378.3 40.4 %all-gather.3.cloned.1.call-done = bf16[3584,640]{1,0:T(8,128)(2,1)} async-done(((bf16[112,640]{1,0:T(8,128)(2,1)}), bf16[3584,640]{1,0:T(8,128)(2,1)}) %all-gather.3.cloned.1.call-update) | async-done | bytes 4587536 | tf_op jit(solution)/shard_map/all_gather | solution.py:85
  418.7 10.3 %convolution_convert_fusion.2 = bf16[1024,640]{1,0:T(8,128)(2,1)} fusion(bf16[1024,3584]{1,0:T(8,128)(2,1)} %bitcast.58, bf16[3584,640]{1,0:T(8,128)(2,1)} %all-gather.3.cloned.1.call-done), kind=kOutput, calls=%fused_computation.12 | convolution fusion | flops 4698275840 | bytes 13238272 | tf_op jit(solution)/shard_map/dot_general | solution.py:83
  (85 shorter events, 52.5 us)
Async XLA Ops:
  24.3 21.9 %copy-start.7 = (s32[1,4]{1,0:T(1,128)S(1)}, s32[1,4]{1,0:T(1,128)}, u32[]{:S(2)}) copy-start(s32[1,4]{1,0:T(1,128)} %param.7) | copy-start | bytes 52
  24.4 21.9 %copy-start.8 = (s32[1,4]{1,0:T(1,128)S(1)}, s32[1,4]{1,0:T(1,128)}, u32[]{:S(2)}) copy-start(s32[1,4]{1,0:T(1,128)} %param.6) | copy-start | bytes 52
  30.4 194.1 %all-to-all-start = ((bf16[16,2,57344]{2,1,0:T(2,128)(2,1)}), bf16[16,2,57344]{2,1,0:T(2,128)(2,1)}, u32[]{:S(2)}, u32[]{:S(2)}) async-start(bf16[16,2,57344]{2,1,0:T(2,128)(2,1)} %reshape.239), calls=%async_computation | async-start | bytes 7340032 | tf_op jit(solution)/shard_map/all_to_all | solution.py:119
  46.2 372.5 %all-gather.3.cloned.1.call-start = ((), (), s32[]{:S(2)}) async-start(), calls=%async_computation.1 | async-start | bytes 4730880 | tf_op jit(solution)/shard_map/all_gather | solution.py:85
  244.1 10.4 %collective-permute-start = (bf16[64,3584]{1,0:T(8,128)(2,1)S(1)}, bf16[64,3584]{1,0:T(8,128)(2,1)S(1)}, u32[]{:S(2)}, u32[]{:S(2)}) collective-permute-start(bf16[64,3584]{1,0:T(8,128)(2,1)S(1)} %reshape.217), channel_id=1, source_target_pairs={{0,32},{32,64},{64,96},{96,128},{128,160},{160,192},{192,224},{224... | collective-permute-start | bytes 1376264 | tf_op jit(solution)/shard_map/ppermute | solution.py:24
  254.6 12.5 %collective-permute-start.1 = (bf16[64,3584]{1,0:T(8,128)(2,1)S(1)}, bf16[64,3584]{1,0:T(8,128)(2,1)S(1)}, u32[]{:S(2)}, u32[]{:S(2)}) collective-permute-start(bf16[64,3584]{1,0:T(8,128)(2,1)S(1)} %collective-permute-done), channel_id=1, source_target_pairs={{0,32},{32,64},{64,96},{96,128},{128,160},{160,192},{192,224},{224... | collective-permute-start | bytes 1376264 | tf_op jit(solution)/shard_map/ppermute | solution.py:24
  256.5 12.5 %collective-permute-start.8 = (bf16[64,3584]{1,0:T(8,128)(2,1)S(1)}, bf16[64,3584]{1,0:T(8,128)(2,1)S(1)}, u32[]{:S(2)}, u32[]{:S(2)}) collective-permute-start(bf16[64,3584]{1,0:T(8,128)(2,1)S(1)} %reshape.217), channel_id=1, source_target_pairs={{32,0},{64,32},{96,64},{128,96},{160,128},{192,160},{224,192},{256... | collective-permute-start | bytes 1376264 | tf_op jit(solution)/shard_map/ppermute | solution.py:26
  267.0 13.6 %collective-permute-start.2 = (bf16[64,3584]{1,0:T(8,128)(2,1)S(1)}, bf16[64,3584]{1,0:T(8,128)(2,1)S(1)}, u32[]{:S(2)}, u32[]{:S(2)}) collective-permute-start(bf16[64,3584]{1,0:T(8,128)(2,1)S(1)} %collective-permute-done.1), channel_id=1, source_target_pairs={{0,32},{32,64},{64,96},{96,128},{128,160},{160,192},{192,224},{224... | collective-permute-start | bytes 1376264 | tf_op jit(solution)/shard_map/ppermute | solution.py:24
  269.0 13.6 %collective-permute-start.9 = (bf16[64,3584]{1,0:T(8,128)(2,1)S(1)}, bf16[64,3584]{1,0:T(8,128)(2,1)S(1)}, u32[]{:S(2)}, u32[]{:S(2)}) collective-permute-start(bf16[64,3584]{1,0:T(8,128)(2,1)S(1)} %collective-permute-done.8), channel_id=1, source_target_pairs={{32,0},{64,32},{96,64},{128,96},{160,128},{192,160},{224,192},{256... | collective-permute-start | bytes 1376264 | tf_op jit(solution)/shard_map/ppermute | solution.py:26
  280.6 14.8 %collective-permute-start.3 = (bf16[64,3584]{1,0:T(8,128)(2,1)S(1)}, bf16[64,3584]{1,0:T(8,128)(2,1)S(1)}, u32[]{:S(2)}, u32[]{:S(2)}) collective-permute-start(bf16[64,3584]{1,0:T(8,128)(2,1)S(1)} %collective-permute-done.2), channel_id=1, source_target_pairs={{0,32},{32,64},{64,96},{96,128},{128,160},{160,192},{192,224},{224... | collective-permute-start | bytes 1376264 | tf_op jit(solution)/shard_map/ppermute | solution.py:24
  282.6 14.8 %collective-permute-start.10 = (bf16[64,3584]{1,0:T(8,128)(2,1)S(1)}, bf16[64,3584]{1,0:T(8,128)(2,1)S(1)}, u32[]{:S(2)}, u32[]{:S(2)}) collective-permute-start(bf16[64,3584]{1,0:T(8,128)(2,1)S(1)} %collective-permute-done.9), channel_id=1, source_target_pairs={{32,0},{64,32},{96,64},{128,96},{160,128},{192,160},{224,192},{256... | collective-permute-start | bytes 1376264 | tf_op jit(solution)/shard_map/ppermute | solution.py:26
  295.4 32.2 %copy-start.4 = (bf16[64,3584]{1,0:T(8,128)(2,1)}, bf16[64,3584]{1,0:T(8,128)(2,1)S(1)}, u32[]{:S(2)}) copy-start(bf16[64,3584]{1,0:T(8,128)(2,1)S(1)} %collective-permute-done.3) | copy-start | bytes 1376260
  295.4 15.1 %collective-permute-start.4 = (bf16[64,3584]{1,0:T(8,128)(2,1)S(1)}, bf16[64,3584]{1,0:T(8,128)(2,1)S(1)}, u32[]{:S(2)}, u32[]{:S(2)}) collective-permute-start(bf16[64,3584]{1,0:T(8,128)(2,1)S(1)} %collective-permute-done.3), channel_id=1, source_target_pairs={{0,32},{32,64},{64,96},{96,128},{128,160},{160,192},{192,224},{224... | collective-permute-start | bytes 1376264 | tf_op jit(solution)/shard_map/ppermute | solution.py:24
  297.3 42.7 %copy-start = (bf16[64,3584]{1,0:T(8,128)(2,1)}, bf16[64,3584]{1,0:T(8,128)(2,1)S(1)}, u32[]{:S(2)}) copy-start(bf16[64,3584]{1,0:T(8,128)(2,1)S(1)} %collective-permute-done.10) | copy-start | bytes 1376260
  297.4 15.0 %collective-permute-start.11 = (bf16[64,3584]{1,0:T(8,128)(2,1)S(1)}, bf16[64,3584]{1,0:T(8,128)(2,1)S(1)}, u32[]{:S(2)}, u32[]{:S(2)}) collective-permute-start(bf16[64,3584]{1,0:T(8,128)(2,1)S(1)} %collective-permute-done.10), channel_id=1, source_target_pairs={{32,0},{64,32},{96,64},{128,96},{160,128},{192,160},{224,192},{256... | collective-permute-start | bytes 1376264 | tf_op jit(solution)/shard_map/ppermute | solution.py:26
  310.5 22.4 %copy-start.5 = (bf16[64,3584]{1,0:T(8,128)(2,1)}, bf16[64,3584]{1,0:T(8,128)(2,1)S(1)}, u32[]{:S(2)}) copy-start(bf16[64,3584]{1,0:T(8,128)(2,1)S(1)} %collective-permute-done.4) | copy-start | bytes 1376260
  310.5 14.2 %collective-permute-start.5 = (bf16[64,3584]{1,0:T(8,128)(2,1)S(1)}, bf16[64,3584]{1,0:T(8,128)(2,1)S(1)}, u32[]{:S(2)}, u32[]{:S(2)}) collective-permute-start(bf16[64,3584]{1,0:T(8,128)(2,1)S(1)} %collective-permute-done.4), channel_id=1, source_target_pairs={{0,32},{32,64},{64,96},{96,128},{128,160},{160,192},{192,224},{224... | collective-permute-start | bytes 1376264 | tf_op jit(solution)/shard_map/ppermute | solution.py:24
  313.2 14.4 %collective-permute-start.12 = (bf16[64,3584]{1,0:T(8,128)(2,1)S(1)}, bf16[64,3584]{1,0:T(8,128)(2,1)}, u32[]{:S(2)}, u32[]{:S(2)}) collective-permute-start(bf16[64,3584]{1,0:T(8,128)(2,1)S(1)} %collective-permute-done.11), channel_id=1, source_target_pairs={{32,0},{64,32},{96,64},{128,96},{160,128},{192,160},{224,192},{256... | collective-permute-start | bytes 1376264 | tf_op jit(solution)/shard_map/ppermute | solution.py:26
  324.7 13.4 %collective-permute-start.6 = (bf16[64,3584]{1,0:T(8,128)(2,1)S(1)}, bf16[64,3584]{1,0:T(8,128)(2,1)}, u32[]{:S(2)}, u32[]{:S(2)}) collective-permute-start(bf16[64,3584]{1,0:T(8,128)(2,1)S(1)} %collective-permute-done.5), channel_id=1, source_target_pairs={{0,32},{32,64},{64,96},{96,128},{128,160},{160,192},{192,224},{224... | collective-permute-start | bytes 1376264 | tf_op jit(solution)/shard_map/ppermute | solution.py:24
  327.6 13.7 %collective-permute-start.13 = (bf16[64,3584]{1,0:T(8,128)(2,1)}, bf16[64,3584]{1,0:T(8,128)(2,1)}, u32[]{:S(2)}, u32[]{:S(2)}) collective-permute-start(bf16[64,3584]{1,0:T(8,128)(2,1)} %collective-permute-done.12), channel_id=1, source_target_pairs={{32,0},{64,32},{96,64},{128,96},{160,128},{192,160},{224,192},{256... | collective-permute-start | bytes 1376264 | tf_op jit(solution)/shard_map/ppermute | solution.py:26
  338.0 13.0 %collective-permute-start.7 = (bf16[64,3584]{1,0:T(8,128)(2,1)}, bf16[64,3584]{1,0:T(8,128)(2,1)}, u32[]{:S(2)}, u32[]{:S(2)}) collective-permute-start(bf16[64,3584]{1,0:T(8,128)(2,1)} %collective-permute-done.6), channel_id=1, source_target_pairs={{0,32},{32,64},{64,96},{96,128},{128,160},{160,192},{192,224},{224... | collective-permute-start | bytes 1376264 | tf_op jit(solution)/shard_map/ppermute | solution.py:24
  340.5 24.6 %copy-start.1 = (bf16[64,3584]{1,0:T(8,128)(2,1)S(1)}, bf16[64,3584]{1,0:T(8,128)(2,1)}, u32[]{:S(2)}) copy-start(bf16[64,3584]{1,0:T(8,128)(2,1)} %copy-done) | copy-start | bytes 1376260
  340.5 25.4 %copy-start.3 = (bf16[64,3584]{1,0:T(8,128)(2,1)S(1)}, bf16[64,3584]{1,0:T(8,128)(2,1)}, u32[]{:S(2)}) copy-start(bf16[64,3584]{1,0:T(8,128)(2,1)} %copy-done.2) | copy-start | bytes 1376260
  341.3 29.1 %collective-permute-start.14 = (bf16[64,3584]{1,0:T(8,128)(2,1)}, bf16[64,3584]{1,0:T(8,128)(2,1)S(1)}, u32[]{:S(2)}, u32[]{:S(2)}) collective-permute-start(bf16[64,3584]{1,0:T(8,128)(2,1)} %collective-permute-done.13), channel_id=1, source_target_pairs={{32,0},{64,32},{96,64},{128,96},{160,128},{192,160},{224,192},{256... | collective-permute-start | bytes 1376264 | tf_op jit(solution)/shard_map/ppermute | solution.py:26
  (2 other events, 14.2 us)
Sparse Core Ops, SparseCore 0:
  340.1 78.5 all-gather.2
